TPU v7x, 128 devices: a whole 4x4x4 slice. The times are simulated.
128 devices in a mesh: row: 16 (over y, x), col: 4 (over z), depth: 2 (over core).
Axes of the slice: x: 4, y: 4, z: 4, core: 2. Of those that a mesh axis runs over, the one named last changes fastest.
Arguments:
- layers: float32 [2, 16384, 16384], P('depth', 'row', 'col'), may hold values from -3 to 265.4, as said below
Outputs:
- factor: float32 [2, 16384, 512], P(None, 'row', 'depth')
- schur: float32 [16384, 16384], P(('row', 'depth'), 'col')
Inputs may be any that keep to these rules, and one draw needn't show every extreme that they name: Read in matrix order, each layer is symmetric, and the sum over layers is symmetric positive definite with a diagonal of order sqrt(16384).
All inputs are finite; a program needn't handle non-finite values.
Results may differ from a plain program's by a relative error of at most 0.0001.
Values sent between devices are 32-bit elements; how exact they have to be, the bound alone decides.
A program may use at most 192 MiB of HBM per device.

v0:
```python
import jax
import jax.numpy as jnp
from jax import lax
from jax.sharding import PartitionSpec as P

PANEL = 512
PANELS = 2


def broadcast(value, axis, source):
    kept = jnp.where(lax.axis_index(axis) == source, value, 0).astype(value.dtype)
    return lax.psum(kept, axis)


def sent_to_all(x, axis):
    devices = lax.axis_size(axis)
    return lax.all_to_all(jnp.broadcast_to(x[None], (devices, *x.shape)), axis, 0, 0, tiled=True)


def of_everyone(x, axis):
    return sent_to_all(x, axis).sum(axis=0)


def cut_along(x, dim, devices):
    before, after = (x.shape[:dim], x.shape[dim + 1 :])
    return jnp.moveaxis(x.reshape(*before, devices, -1, *after), dim, 0)


def summed_on_arrival(x, axis, dim):
    devices = lax.axis_size(axis)
    tiles = lax.all_to_all(cut_along(x, dim, devices), axis, 0, 0, tiled=True)
    return jnp.sum(tiles, axis=0)


def broadcast_2(x, axis, root):
    return lax.dynamic_index_in_dim(lax.all_gather(x, axis), root, 0, keepdims=False)


def block_inverse(diagonal, identity_block):
    lower_diag = jnp.linalg.cholesky(diagonal)
    return jax.scipy.linalg.solve_triangular(lower_diag, identity_block, lower=True)


def outer_update(left_rows, right_rows):
    return lax.dot_general(
        left_rows,
        right_rows,
        (((1,), (1,)), ((), ())),
        precision=lax.Precision.HIGHEST,
        preferred_element_type=jnp.float32,
    )


def per_device(layers):
    row_groups = lax.axis_size("row")
    col_groups = lax.axis_size("col")
    depth_groups = lax.axis_size("depth")
    row_index = lax.axis_index("row")
    col_index = lax.axis_index("col")
    depth_index = lax.axis_index("depth")
    layer_part = layers[0]
    rows_local = layer_part.shape[0]
    cols_local = layer_part.shape[1]
    slice_width = PANEL // depth_groups
    quarter_rows = rows_local // depth_groups
    local_blocks = rows_local // PANEL
    row_block = jnp.arange(rows_local, dtype=jnp.int32) // PANEL * row_groups + row_index
    col_block = jnp.arange(cols_local, dtype=jnp.int32) // PANEL * col_groups + col_index
    identity_block = jnp.eye(PANEL, dtype=jnp.float32)
    factor_list = []
    schur = None
    for panel_step in range(PANELS):
        owner_col = panel_step % col_groups
        local_col = panel_step // col_groups
        owner_row = panel_step % row_groups
        local_row = panel_step // row_groups
        column = layer_part[:, local_col * PANEL : (local_col + 1) * PANEL]
        layer_diag = broadcast(
            column[local_row * PANEL : (local_row + 1) * PANEL], "row", owner_row
        )
        diagonal = of_everyone(layer_diag, "depth")
        quarter = summed_on_arrival(column, "depth", 0)
        inverse = block_inverse(diagonal, identity_block)
        solved = jnp.dot(quarter, inverse.T, precision=lax.Precision.HIGHEST)
        quarter_block = lax.dynamic_slice_in_dim(
            row_block, depth_index * quarter_rows, quarter_rows, 0
        )
        solved = jnp.where(quarter_block[:, None] >= panel_step, solved, 0.0)
        row_slice = lax.all_to_all(solved, "depth", split_axis=1, concat_axis=0, tiled=True)
        panel_rows = broadcast_2(row_slice, "col", owner_col)
        factor_list.append(panel_rows)
        update_rows = jnp.where(row_block[:, None] > panel_step, panel_rows, 0.0)
        gathered = lax.all_gather(panel_rows, "row", axis=0, tiled=True)
        grouped = gathered.reshape(
            row_groups // col_groups, col_groups, local_blocks, PANEL, slice_width
        )
        picked = lax.dynamic_index_in_dim(grouped, col_index, 1, keepdims=False)
        column_rows = picked.transpose(1, 0, 2, 3).reshape(cols_local, slice_width)
        update_cols = jnp.where(col_block[:, None] > panel_step, column_rows, 0.0)
        if panel_step + 1 < PANELS:
            layer_part = layer_part - outer_update(update_rows, update_cols)
        else:
            schur = summed_on_arrival(
                layer_part - outer_update(update_rows, update_cols), "depth", 0
            )
    return (jnp.stack(factor_list), schur)


def solution(mesh):
    return jax.shard_map(
        per_device,
        mesh=mesh,
        in_specs=(P("depth", "row", "col"),),
        out_specs=(P(None, "row", "depth"), P(("row", "depth"), "col")),
        check_vma=False,
    )
```

profile of v0, /device:TPU:1, one launch (start us, length us, event | category | flops | bytes accessed | tf_op | source)
XLA Modules:
  0.0 959.5 jit_solution(3367410215411466751)
XLA Ops:
  7.2 17.5 %copy.41 = f32[1,1024,4096]{1,2,0:T(8,128)} copy(f32[1,1024,4096]{2,1,0:T(8,128)} %param.4) | data formatting | bytes 33554432 | tf_op args[0]
  39.3 76.7 %all-reduce.4.cloned.1.call-done = f32[512,512]{0,1:T(8,128)} async-done(((f32[512,512]{0,1:T(8,128)}), f32[512,512]{0,1:T(8,128)}) %all-reduce.4.cloned.1.call-update) | async-done | bytes 1048592 | tf_op jit(solution)/shard_map/psum | solution.py:12
  129.4 11.7 %cholesky.286 = f32[128,128]{1,0:T(8,128)S(1)} custom-call(f32[128,128]{1,0:T(8,128)S(1)} %cholesky.426), custom_call_target="Cholesky" | custom-call | tf_op jit(solution)/shard_map/jit(cholesky)/cholesky | solution.py:40
  153.6 11.7 %cholesky.305 = f32[128,128]{1,0:T(8,128)S(1)} custom-call(f32[128,128]{1,0:T(8,128)S(1)} %cholesky.430), custom_call_target="Cholesky" | custom-call | tf_op jit(solution)/shard_map/jit(cholesky)/cholesky | solution.py:40
  165.4 10.1 %custom-call.28 = f32[1,128,128]{1,2,0:T(8,128)S(1)} custom-call(f32[1,128,128]{2,1,0:T(8,128)S(1)} %get-tuple-element.60), custom_call_target="InvertDiagBlocksLowerTriangular" | custom-call | tf_op jit(solution)/shard_map/jit(cholesky)/cholesky | solution.py:40
  177.1 11.7 %cholesky.326 = f32[128,128]{1,0:T(8,128)S(1)} custom-call(f32[128,128]{1,0:T(8,128)S(1)} %cholesky.435), custom_call_target="Cholesky" | custom-call | tf_op jit(solution)/shard_map/jit(cholesky)/cholesky | solution.py:40
  200.7 11.9 %cholesky.343 = f32[128,128]{1,0:T(8,128)S(1)} custom-call(f32[128,128]{1,0:T(8,128)S(1)} %convolution_subtract_fusion.13), custom_call_target="Cholesky" | custom-call | tf_op jit(solution)/shard_map/jit(cholesky)/cholesky | solution.py:40
  217.7 11.7 %while.4 = (s32[]{:T(128)}, f32[512,512]{1,0:T(8,128)}, s32[4,2]{0,1:T(2,128)S(1)}, f32[4,128,128]{2,1,0:T(8,128)S(1)}, s32[]{:T(128)}) while((s32[]{:T(128)}, f32[512,512]{1,0:T(8,128)}, s32[4,2]{0,1:T(2,128)S(1)}, f32[4,128,128]{2,1,0:T(8,128)S(1)}, s32[]{:T(128)}) %tuple.58), condition=%wide.while_cond, body=%wide.while_body.sunk | while | flops 2 | bytes 131181 | solution.py:41
  229.3 39.3 %custom-call.30 = f32[4,128,128]{1,2,0:T(8,128)S(1)} custom-call(f32[4,128,128]{2,1,0:T(8,128)S(1)} %get-tuple-element.18), custom_call_target="InvertDiagBlocksLowerTriangular" | custom-call | tf_op jit(solution)/shard_map/jit(_solve_triangular)/triangular_solve | solution.py:41
  282.4 47.3 %all-gather.7.cloned.1.call-done = f32[4,1024,256]{2,1,0:T(8,128)} async-done(((f32[1,1024,256]{2,1,0:T(8,128)}), f32[4,1024,256]{2,1,0:T(8,128)}) %all-gather.7.cloned.1.call-update) | async-done | bytes 4194320 | tf_op jit(solution)/shard_map/all_gather | solution.py:36
  332.1 111.6 %all-gather.11.cloned.1.call-done = f32[1,16384,256]{2,1,0:T(8,128)} async-done(((f32[1,1024,256]{2,1,0:T(8,128)}), f32[1,16384,256]{2,1,0:T(8,128)}) %all-gather.11.cloned.1.call-update) | async-done | bytes 16777232 | tf_op jit(solution)/shard_map/all_gather | solution.py:93
  446.9 19.2 %convolution_subtract_fusion.1 = f32[1024,4096]{0,1:T(8,128)} fusion(f32[4096,256]{1,0:T(8,128)S(1)} %bitcast.148, pred[1024]{0:T(1024)(128)(4,1)S(1)} %broadcast_compare_fusion.2, f32[1,1024,4096]{1,2,0:T(8,128)} %copy.41, f32[4,1024,256]{2,1,0:T(8,128)} %all-gather.7.cloned.1.call-done), kind=kOutput, calls=%fused_computation.6 | convolution fusion | flops 12889358336 | bytes 38798336 | tf_op jit(solution)/shard_map/dot_general | solution.py:45
  476.0 78.3 %all-reduce.6.cloned.1.call-done = f32[512,512]{0,1:T(8,128)} async-done(((f32[512,512]{0,1:T(8,128)}), f32[512,512]{0,1:T(8,128)}) %all-reduce.6.cloned.1.call-update) | async-done | bytes 1048592 | tf_op jit(solution)/shard_map/psum | solution.py:12
  567.7 11.7 %cholesky.358 = f32[128,128]{1,0:T(8,128)S(1)} custom-call(f32[128,128]{1,0:T(8,128)S(1)} %cholesky.439), custom_call_target="Cholesky" | custom-call | tf_op jit(solution)/shard_map/jit(cholesky)/cholesky | solution.py:40
  591.9 11.7 %cholesky.377 = f32[128,128]{1,0:T(8,128)S(1)} custom-call(f32[128,128]{1,0:T(8,128)S(1)} %cholesky.443), custom_call_target="Cholesky" | custom-call | tf_op jit(solution)/shard_map/jit(cholesky)/cholesky | solution.py:40
  616.6 11.7 %cholesky.398 = f32[128,128]{1,0:T(8,128)S(1)} custom-call(f32[128,128]{1,0:T(8,128)S(1)} %cholesky.448), custom_call_target="Cholesky" | custom-call | tf_op jit(solution)/shard_map/jit(cholesky)/cholesky | solution.py:40
  640.3 11.9 %cholesky.415 = f32[128,128]{1,0:T(8,128)S(1)} custom-call(f32[128,128]{1,0:T(8,128)S(1)} %convolution_subtract_fusion.12), custom_call_target="Cholesky" | custom-call | tf_op jit(solution)/shard_map/jit(cholesky)/cholesky | solution.py:40
  656.4 11.7 %while.5 = (s32[]{:T(128)}, f32[512,512]{1,0:T(8,128)}, s32[4,2]{0,1:T(2,128)S(1)}, f32[4,128,128]{2,1,0:T(8,128)S(1)}, s32[]{:T(128)}) while((s32[]{:T(128)}, f32[512,512]{1,0:T(8,128)}, s32[4,2]{0,1:T(2,128)S(1)}, f32[4,128,128]{2,1,0:T(8,128)S(1)}, s32[]{:T(128)}) %tuple.76), condition=%wide.while_cond.clone, body=%wide.while_body.clone.sunk | while | flops 2 | bytes 131181 | solution.py:41
  668.1 39.3 %custom-call.34 = f32[4,128,128]{1,2,0:T(8,128)S(1)} custom-call(f32[4,128,128]{2,1,0:T(8,128)S(1)} %get-tuple-element.19), custom_call_target="InvertDiagBlocksLowerTriangular" | custom-call | tf_op jit(solution)/shard_map/jit(_solve_triangular)/triangular_solve | solution.py:41
  721.3 47.3 %all-gather.9.cloned.1.call-done = f32[4,1024,256]{2,1,0:T(8,128)} async-done(((f32[1,1024,256]{2,1,0:T(8,128)}), f32[4,1024,256]{2,1,0:T(8,128)}) %all-gather.9.cloned.1.call-update) | async-done | bytes 4194320 | tf_op jit(solution)/shard_map/all_gather | solution.py:36
  773.6 108.8 %all-gather.13.cloned.1.call-done = f32[1,16384,256]{2,1,0:T(8,128)} async-done(((f32[1,1024,256]{2,1,0:T(8,128)}), f32[1,16384,256]{2,1,0:T(8,128)}) %all-gather.13.cloned.1.call-update) | async-done | bytes 16777232 | tf_op jit(solution)/shard_map/all_gather | solution.py:93
  885.9 19.2 %convolution_subtract_fusion = f32[1024,4096]{0,1:T(8,128)} fusion(f32[1024,4096]{0,1:T(8,128)} %convolution_subtract_fusion.1, f32[4096,256]{1,0:T(8,128)S(1)} %bitcast.147, pred[1024]{0:T(1024)(128)(4,1)S(1)} %broadcast_compare_fusion.3, f32[4,1024,256]{2,1,0:T(8,128)} %all-gather.9.cloned.1.call-done), kind=kOutput, calls=%fused_computation.5 | convolution fusion | flops 12889358336 | bytes 38798336 | tf_op jit(solution)/shard_map/dot_general | solution.py:45
  911.9 19.5 %all_to_all.62 = f32[2,512,4096]{1,2,0:T(8,128)} all-to-all(f32[2,512,4096]{1,2,0:T(8,128)S(1)} %bitcast.146), channel_id=1, replica_groups=mesh['row'=16,'col'=4,'depth'=2] {'depth'}, dimensions={0} | all-to-all | bytes 33554432 | tf_op jit(solution)/shard_map/all_to_all | solution.py:31
  931.4 11.9 %reduce_sum.49 = f32[512,4096]{0,1:T(8,128)} reduce(f32[2,512,4096]{1,2,0:T(8,128)} %all_to_all.62, f32[]{:T(128)} %constant.194.clone.1), dimensions={0}, to_apply=%region_14.17 | reduce | flops 2097152 | bytes 25165828 | tf_op jit(solution)/shard_map/reduce_sum | solution.py:32
  (150 shorter events, 199.4 us)
Async XLA Ops:
  7.2 108.8 %all-reduce.4.cloned.1.call-start = ((), (), s32[]{:S(2)}) async-start(), calls=%async_computation.7 | async-start | bytes 2097152 | tf_op jit(solution)/shard_map/psum | solution.py:12
  30.2 7.6 all-to-all-start
  35.4 294.3 %all-gather.7.cloned.1.call-start = ((), (), s32[]{:S(2)}) async-start(), calls=%async_computation.8 | async-start | bytes 5242880 | tf_op jit(solution)/shard_map/all_gather | solution.py:36
  128.4 1.0 copy-start.4
  216.5 58.0 %copy-start.1 = (f32[512,512]{0,1:T(8,128)S(1)}, f32[512,512]{0,1:T(8,128)}, u32[]{:S(2)}) copy-start(f32[512,512]{0,1:T(8,128)} %reduce_sum.45) | copy-start | bytes 3145732
  282.3 161.3 %all-gather.11.cloned.1.call-start = ((), (), s32[]{:S(2)}) async-start(), calls=%async_computation.11 | async-start | bytes 17825792 | tf_op jit(solution)/shard_map/all_gather | solution.py:93
  331.9 222.3 %all-reduce.6.cloned.1.call-start = ((), (), s32[]{:S(2)}) async-start(), calls=%async_computation.9 | async-start | bytes 2097152 | tf_op jit(solution)/shard_map/psum | solution.py:12
  466.1 2.6 slice-start
  468.6 300.0 %all-gather.9.cloned.1.call-start = ((), (), s32[]{:S(2)}) async-start(), calls=%async_computation.10 | async-start | bytes 5242880 | tf_op jit(solution)/shard_map/all_gather | solution.py:36
  566.7 1.0 copy-start.3
  655.3 58.0 %copy-start.2 = (f32[512,512]{0,1:T(8,128)S(1)}, f32[512,512]{0,1:T(8,128)}, u32[]{:S(2)}) copy-start(f32[512,512]{0,1:T(8,128)} %reduce_sum.47) | copy-start | bytes 3145732
  715.2 55.7 %copy-start = (f32[1,1024,256]{2,1,0:T(8,128)S(1)}, f32[1,1024,256]{2,1,0:T(8,128)}, u32[]{:S(2)}) copy-start(f32[1,1024,256]{2,1,0:T(8,128)} %dynamic_slice.23) | copy-start | bytes 3145732
  721.2 161.2 %all-gather.13.cloned.1.call-start = ((), (), s32[]{:S(2)}) async-start(), calls=%async_computation.12 | async-start | bytes 17825792 | tf_op jit(solution)/shard_map/all_gather | solution.py:93
Sparse Core Ops, SparseCore 0:
  27.1 88.8 all-reduce.3
  282.5 47.1 all-gather.6
  332.4 111.2 all-gather.10
  468.7 85.4 all-reduce.5
  721.4 47.1 all-gather.8
  771.1 111.2 all-gather.12
where the time goes:
time: 972 us; the launch traced here: 960 us
  waiting for transfers between devices  473 us (49%)
  other arithmetic  272 us (28%)
  local copies, waits for them, and re-layouts  73.5 us (8%)
  matrix products  64.6 us (7%)
  blocking collectives  51 us (5%)
  between operations  20.1 us (2%)
    all_gather x2, waiting for transfers between devices, per_device(): gathered = lax.all_gather(panel_rows, 'row', axis=0, tiled=True)  220 us
    another operation x29, other arithmetic, block_inverse(): lower_diag = jnp.linalg.cholesky(diagonal)  158 us
    psum x2, waiting for transfers between devices, broadcast(): return lax.psum(kept, axis)  155 us
    all_gather x2, waiting for transfers between devices, broadcast_2(): lax.all_gather(x, axis)  94.5 us
    another operation x5, other arithmetic, block_inverse(): jax.scipy.linalg.solve_triangular(lower_diag, identity_block, lower=True)  80.9 us
    dot_general x2, matrix products, outer_update(): lax.dot_general(left_rows, right_rows, (((1,), (1,)), ((), ())), precisio...  38.3 us
    unnamed x12, local copies, waits for them, and re-layouts  28.3 us
    all_to_all x2, blocking collectives, summed_on_arrival(): tiles = lax.all_to_all(cut_along(x, dim, devices), axis, 0, 0, tiled=True)  25.4 us
  transfers between devices with their start and end apart: 7, of which 7 were waited for; matrix products, arithmetic and copies ran while one was open for 1% of the time, Pallas kernels for 0%

commit v1 on v0

v1 whole, which is shorter than its diff:
```python
import jax
import jax.numpy as jnp
from jax import lax
from jax.experimental import pallas as pl
from jax.experimental.pallas import tpu as pltpu
from jax.sharding import PartitionSpec as P

PANEL = 512
BLOCK = 128
HI = lax.Precision.HIGHEST
MESH = pl.DeviceIdType.MESH
F32 = jnp.float32


def inverse_factor(x):
    n = x.shape[0]
    lane8 = lax.broadcasted_iota(jnp.int32, (8, n), 1)
    sub8 = lax.broadcasted_iota(jnp.int32, (8, n), 0)
    out = []
    for k in range(n // 8):
        lo = 8 * k
        head, rest = x[:8], x[8:]
        ck = [jnp.broadcast_to(head[:, lo + j : lo + j + 1], (8, n)) for j in range(8)]
        inblk = (lane8 >= lo) & (lane8 < lo + 8)
        head = jnp.where(inblk, jnp.where(lane8 - lo == sub8, 1.0, 0.0), head)
        more = rest.shape[0] > 0
        if more:
            cr = [jnp.broadcast_to(rest[:, lo + j : lo + j + 1], rest.shape) for j in range(8)]
            lane = lax.broadcasted_iota(jnp.int32, rest.shape, 1)
            rest = jnp.where((lane >= lo) & (lane < lo + 8), 0.0, rest)
        pivots = ck[0]
        for j in range(8):
            if j:
                pivots = jnp.where(sub8 == j, ck[j], pivots)
            inv = 1.0 / ck[j][j : j + 1, :]
            mk = jnp.where(sub8 > j, ck[j], 0.0) * inv
            if more:
                mr = cr[j] * inv
            for t in range(j + 1, 8):
                row = ck[t][j : j + 1, :]
                ck[t] = ck[t] - mk * row
                if more:
                    cr[t] = cr[t] - mr * row
            row = head[j : j + 1, :]
            head = head - mk * row
            if more:
                rest = rest - mr * row
        out.append(jnp.where(lane8 <= sub8 + lo, head, 0.0) * lax.rsqrt(pivots))
        x = rest
    return jnp.concatenate(out, axis=0)


def factor_steps(v_ref, urow):
    size = v_ref.shape[0]
    blocks = size // BLOCK

    def step(j, carry):
        off = pl.multiple_of(j * BLOCK, BLOCK)
        here = pl.ds(off, BLOCK)
        w = inverse_factor(v_ref[here, here])
        urow[...] = jnp.dot(w, v_ref[here, :], precision=HI, preferred_element_type=F32)
        urow[:, here] = w
        for i in range(1, blocks):

            @pl.when(i > j)
            def _():
                rows = pl.ds(i * BLOCK, BLOCK)
                v_ref[rows, here] = jnp.zeros((BLOCK, BLOCK), F32)
                v_ref[rows, :] -= lax.dot_general(
                    urow[:, rows],
                    urow[...],
                    (((0,), (0,)), ((), ())),
                    precision=HI,
                    preferred_element_type=F32,
                )

        lane = lax.broadcasted_iota(jnp.int32, (BLOCK, size), 1)
        v_ref[here, :] = jnp.where(lane < off + BLOCK, urow[...], 0.0)
        return carry

    lax.fori_loop(0, blocks, step, 0)


def factor_kernel(d_ref, v_ref, urow):
    v_ref[:PANEL, :PANEL] = d_ref[0]
    v_ref[:PANEL, PANEL:] = d_ref[1]
    v_ref[PANEL:, :PANEL] = jnp.zeros((PANEL, PANEL), F32)
    v_ref[PANEL:, PANEL:] = d_ref[2]
    factor_steps(v_ref, urow)


def inverse_cholesky(d):
    size = 2 * PANEL
    return pl.pallas_call(
        factor_kernel,
        out_shape=jax.ShapeDtypeStruct((size, size), F32),
        in_specs=[pl.BlockSpec(memory_space=pltpu.VMEM)],
        out_specs=pl.BlockSpec(memory_space=pltpu.VMEM),
        scratch_shapes=[pltpu.VMEM((BLOCK, size), F32)],
        compiler_params=pltpu.CompilerParams(vmem_limit_bytes=32 * 2**20),
        name="factor",
    )(d)


ORDERS = ((2, 1, 0), (0, 2, 1), (1, 0, 2))
SOURCES = ((0, 0, 0), (0, 0, 1), (1, 0, 1))


def gather_kernel(layer, d_out, g_out, o_out, theirs, q, sem):
    (swap_s, swap_r, half_s, dsc_s, dsc_r, dph_s, dph_r, dsw_s, dsw_r,
     sc_s, sc_r, own_s, own_r, ag_s, ag_r) = sem
    r = lax.axis_index("row")
    z = lax.axis_index("col")
    d = lax.axis_index("depth")
    x = lax.rem(r, 4)
    y = lax.div(r, 4)
    here = (x, y, z)

    def device(c, depth):
        return (c[1] * 4 + c[0], c[2], depth)

    def remote(src, dst, send, recv, target):
        return pltpu.make_async_remote_copy(
            src_ref=src, dst_ref=dst, send_sem=send, recv_sem=recv, device_id=target, device_id_type=MESH
        )

    def moved(axis, by):
        c = list(here)
        c[axis] = lax.rem(c[axis] + by, 4)
        return tuple(c)

    mine = pl.ds(pl.multiple_of(d * PANEL, PANEL), PANEL)
    other = pl.ds(pl.multiple_of((1 - d) * PANEL, PANEL), PANEL)
    cols = pl.ds(0, PANEL)
    swap = remote(layer.at[other, cols], theirs, swap_s, swap_r, device(here, 1 - d))
    swap.start()
    local = pltpu.make_async_copy(layer.at[mine, cols], q, half_s)
    local.start()
    local.wait()
    swap.wait()
    q[...] = q[...] + theirs[...]

    half = PANEL // 2
    for b in range(3):
        sx, sy, sz = SOURCES[b]
        a1, a2, a3 = ORDERS[b]

        @pl.when((x == sx) & (y == sy) & (z == sz) & (d == 0))
        def _():
            def send(i, carry):
                c = [None] * 3
                piece = lax.div(i, 2)
                depth = lax.rem(i, 2)
                c[a1] = lax.rem(piece, 4)
                c[a2] = lax.rem(lax.div(piece, 4), 4)
                c[a3] = lax.div(piece, 16)
                rows = pl.ds(pl.multiple_of(piece * 8, 8), 8)
                part = pl.ds(pl.multiple_of(depth * half, half), half)
                own = (c[0] == sx) & (c[1] == sy) & (c[2] == sz) & (depth == 0)

                @pl.when(jnp.logical_not(own))
                def _():
                    remote(q.at[rows, part], d_out.at[b, rows, part], dsc_s.at[b], dsc_r.at[b], device(c, depth)).start()

                @pl.when(own)
                def _():
                    pltpu.make_async_copy(q.at[rows, part], d_out.at[b, rows, part], dsc_r.at[b]).start()

                return carry

            lax.fori_loop(0, 128, send, 0)

    for p in range(2):

        @pl.when(z == p)
        def _():
            for k in range(4):
                rows = pl.ds(k * BLOCK, BLOCK)
                target = g_out.at[y, k, :, pl.ds(p * PANEL, PANEL)]
                own = (x == p) & (x == k)

                @pl.when(jnp.logical_not(own))
                def _():
                    remote(q.at[rows, :], target, sc_s.at[k], sc_r.at[p], device((k, y, x), d)).start()

                @pl.when(own)
                def _():
                    pltpu.make_async_copy(q.at[rows, :], target, sc_r.at[p]).start()

    part = pl.ds(pl.multiple_of(d * half, half), half)

    def region(b, phase):
        a1, a2, a3 = ORDERS[b]
        c = here
        if phase == 0:
            return c[a3] * 128 + c[a2] * 32 + c[a1] * 8, 8
        if phase == 1:
            return c[a3] * 128 + c[a2] * 32, 32
        return c[a3] * 128, 128

    def phase_copy(b, phase, by):
        start, rows = region(b, phase)
        ref = d_out.at[b, pl.ds(pl.multiple_of(start, rows), rows), part]
        return remote(
            ref, ref, dph_s.at[b, phase, by - 1], dph_r.at[b, phase, by - 1], device(moved(ORDERS[b][phase], by), d)
        )

    def sized(ref, s):
        return pltpu.make_async_copy(ref, ref, s)

    for b in range(3):
        sized(d_out.at[b, pl.ds(0, 8), pl.ds(0, half)], dsc_r.at[b]).wait()
        for by in (1, 2, 3):
            phase_copy(b, 0, by).start()
    for phase in (1, 2):
        for b in range(3):
            for by in (1, 2, 3):
                phase_copy(b, phase - 1, by).wait_recv()
            for by in (1, 2, 3):
                phase_copy(b, phase, by).start()
    for b in range(3):
        for by in (1, 2, 3):
            phase_copy(b, 2, by).wait_recv()

        ref = d_out.at[b, :, part]
        remote(ref, ref, dsw_s.at[b], dsw_r.at[b], device(here, 1 - d)).start()

    def own_copy(p, to, slot):
        src = q
        return remote(src, o_out.at[p], own_s.at[slot], own_r.at[p], device((x, y, to), d))

    for p in range(2):

        @pl.when(z == p)
        def _():
            pltpu.make_async_copy(q, o_out.at[p], own_r.at[p]).start()
            own_copy(p, 1 - p, 0).start()
            own_copy(p, 3 - p, 1).start()

    for b in range(3):
        ref = d_out.at[b, :, part]
        remote(ref, ref, dsw_s.at[b], dsw_r.at[b], device(here, 1 - d)).wait()
        for phase in range(3):
            for by in (1, 2, 3):
                phase_copy(b, phase, by).wait_send()
        sx, sy, sz = SOURCES[b]

        @pl.when((x == sx) & (y == sy) & (z == sz) & (d == 0))
        def _():
            sized(layer.at[pl.ds(0, 127 * 8), pl.ds(0, half)], dsc_s.at[b]).wait()

    def ag_ref(h, phase, c, piece):
        cx, cy = c
        part = pl.ds(h * PANEL, PANEL)
        if phase == 0:
            rows = {None: pl.ds(0, 128), 0: pl.ds(0, 64), 1: pl.ds(64, 64)}[piece]
            return g_out.at[cy, cx, rows, part]
        span = {None: pl.ds(0, 4), 0: pl.ds(0, 2), 1: pl.ds(2, 2)}[piece]
        if h == 0:
            return g_out.at[cy, span, :, part]
        return g_out.at[span, cx, :, part]

    def ag_copy(h, phase, stage, way):
        axis = (phase + h) % 2
        by = 1 if way == 0 else 3
        c = here if stage == 0 else moved(axis, 4 - by)
        ref = ag_ref(h, phase, (c[0], c[1]), None if stage == 0 else way)
        slot = ((h * 2 + phase) * 2 + stage) * 2 + way
        return remote(ref, ref, ag_s.at[slot], ag_r.at[slot], device(moved(axis, by), d))

    for h in range(2):
        sized(g_out.at[0, 0, :, pl.ds(0, PANEL)], sc_r.at[h]).wait()
        for way in range(2):
            ag_copy(h, 0, 0, way).start()
    for phase in range(2):
        for h in range(2):
            for way in range(2):
                ag_copy(h, phase, 0, way).wait_recv()
            for way in range(2):
                ag_copy(h, phase, 1, way).start()
        for h in range(2):
            for way in range(2):
                ag_copy(h, phase, 1, way).wait_recv()
            if phase == 0:
                for way in range(2):
                    ag_copy(h, 1, 0, way).start()
        if phase == 0:
            for p in range(2):

                @pl.when(z == 3 - p)
                def _():
                    sized(o_out.at[p], own_r.at[p]).wait()
                    ref = o_out.at[p]
                    remote(ref, ref, own_s.at[0], own_r.at[p], device((x, y, 2 + p), d)).start()

    for p in range(2):

        @pl.when(z != 3 - p)
        def _():
            sized(o_out.at[p], own_r.at[p]).wait()

    for h in range(2):
        for phase in range(2):
            for stage in range(2):
                for way in range(2):
                    ag_copy(h, phase, stage, way).wait_send()

    @pl.when(z < 2)
    def _():
        sized(q, own_s.at[0]).wait()
        sized(q, own_s.at[1]).wait()

    @pl.when(z >= 2)
    def _():
        sized(q, own_s.at[0]).wait()

    for k in range(4):

        @pl.when((z < 2) & jnp.logical_not((x == z) & (x == k)))
        def _():
            sized(q.at[pl.ds(0, BLOCK), :], sc_s.at[k]).wait()


def gather_panels(layer):
    dma = pltpu.SemaphoreType.DMA
    return pl.pallas_call(
        gather_kernel,
        out_shape=[
            jax.ShapeDtypeStruct((3, PANEL, PANEL), F32),
            jax.ShapeDtypeStruct((4, 4, BLOCK, 2 * PANEL), F32),
            jax.ShapeDtypeStruct((2, PANEL, PANEL), F32),
        ],
        in_specs=[pl.BlockSpec(memory_space=pl.ANY)],
        out_specs=[
            pl.BlockSpec(memory_space=pltpu.VMEM),
            pl.BlockSpec(memory_space=pl.ANY),
            pl.BlockSpec(memory_space=pl.ANY),
        ],
        scratch_shapes=[
            pltpu.VMEM((PANEL, PANEL), F32),
            pltpu.VMEM((PANEL, PANEL), F32),
            (dma, dma, dma, dma((3,)), dma((3,)), dma((3, 3, 3)), dma((3, 3, 3)), dma((3,)), dma((3,)),
             dma((4,)), dma((2,)), dma((2,)), dma((2,)), dma((16,)), dma((16,))),
        ],
        compiler_params=pltpu.CompilerParams(has_side_effects=True, vmem_limit_bytes=24 * 2**20),
        name="gather",
    )(layer)


def product(a, b, precision=lax.Precision.HIGH):
    return lax.dot_general(a, b, (((1,), (1,)), ((), ())), precision=precision, preferred_element_type=F32)


def solved(a0, a1, v, precision):
    c0 = product(a0, v[:PANEL, :PANEL], precision)
    c1 = product(a0, v[PANEL:, :PANEL], precision) + product(a1, v[PANEL:, PANEL:], precision)
    return c0, c1


def per_device(layers):
    r = lax.axis_index("row")
    z = lax.axis_index("col")
    d = lax.axis_index("depth")
    layer = layers[0]
    lead, column_rows, own_rows = gather_panels(layer)
    v = inverse_cholesky(lead)
    g = column_rows.reshape(4 * PANEL, 2 * PANEL)
    swap = [(0, 1), (1, 0)]

    c0, c1 = solved(own_rows[0], own_rows[1], v, HI)
    block = r + 16 * d
    c1 = jnp.where(block >= 1, c1, 0.0)
    own = jnp.concatenate([c0, c1], axis=1)
    peer = lax.ppermute(own, "depth", swap)
    both = jnp.where(d == 0, jnp.stack([own, peer]), jnp.stack([peer, own])).reshape(2 * PANEL, 2 * PANEL)
    half = PANEL // 2
    factor = jnp.stack(
        [jnp.where(d == 0, both[:, p * PANEL : p * PANEL + half], both[:, p * PANEL + half : (p + 1) * PANEL]) for p in range(2)]
    )

    row_block = jnp.arange(2 * PANEL, dtype=jnp.int32) // PANEL * 16 + r
    panel = jnp.arange(2 * PANEL, dtype=jnp.int32) // PANEL
    left = jnp.where(row_block[:, None] > panel[None, :], both, 0.0)
    k0, k1 = solved(g[:, :PANEL], g[:, PANEL:], v, lax.Precision.HIGH)
    col_block = (jnp.arange(4 * PANEL, dtype=jnp.int32) // PANEL + 4 * d) * 4 + z
    right = jnp.where(col_block[:, None] > panel[None, :], jnp.concatenate([k0, k1], axis=1), 0.0)

    width = 4 * PANEL
    near = lax.dynamic_slice_in_dim(layer, d * width, width, 1)
    rows_peer = (1 - d) * PANEL
    far_peer = lax.dynamic_slice(layer, (rows_peer, (1 - d) * width), (PANEL, width))
    far_mine = lax.dynamic_slice(layer, (d * PANEL, (1 - d) * width), (PANEL, width))
    raw = lax.ppermute(far_peer, "depth", swap)
    updated = near - product(left, right)
    sent = lax.dynamic_slice_in_dim(updated, rows_peer, PANEL, 0)
    kept = lax.dynamic_slice_in_dim(updated, d * PANEL, PANEL, 0)
    got = lax.ppermute(sent, "depth", swap)
    here = kept + raw
    there = far_mine + got
    schur = jnp.where(d == 0, jnp.concatenate([here, there], axis=1), jnp.concatenate([there, here], axis=1))
    return factor, schur


def solution(mesh):
    return jax.shard_map(
        per_device,
        mesh=mesh,
        in_specs=(P("depth", "row", "col"),),
        out_specs=(P(None, "row", "depth"), P(("row", "depth"), "col")),
        check_vma=False,
    )
```

time: 972 us -> 258 us (0.27); the launches traced: 960 us -> 258 us
  waiting for transfers between devices: 473 us -> 5.4 us
  other arithmetic: 272 us -> 21.7 us
  Pallas kernels: 0 us -> 154 us
  local copies, waits for them, and re-layouts: 73.5 us -> 21.2 us
  blocking collectives: 51 us -> 0 us
  between operations: 20.1 us -> 0.76 us
  matrix products: 64.6 us -> 50.3 us
    all_gather x4 -> x0, waiting for transfers between devices: 315 us -> none  [the longest x2 220 us: per_device(): gathered = lax.all_gather(panel_rows, 'row', axis=0, tiled=True)]
    another operation x35 -> x3, other arithmetic: 242 us -> 3.58 us  [the longest x1 1.85 us: per_device(): jnp.stack([own, peer])]
    psum x2 -> x0, waiting for transfers between devices: 155 us -> none  [broadcast(): return lax.psum(kept, axis)]
    pallas_call x0 -> x2, Pallas kernels: none -> 154 us  [the longest x1 102 us: gather_panels(): pl.pallas_call(gather_kernel, out_shape=[jax.ShapeDtypeStruct((3, PANEL,...]
    all_to_all x6 -> x0, blocking collectives: 51 us -> none  [the longest x2 25.4 us: summed_on_arrival(): tiles = lax.all_to_all(cut_along(x, dim, devices), axis, 0, 0, tiled=True)]
    another operation x35 -> x0, local copies, waits for them, and re-layouts: 23.5 us -> none  [the longest x27 23.2 us: block_inverse(): jax.scipy.linalg.solve_triangular(lower_diag, identity_block, lower=True)]
    another operation x26 -> x0, matrix products: 22.5 us -> none  [the longest x14 11.6 us: block_inverse(): jax.scipy.linalg.solve_triangular(lower_diag, identity_block, lower=True)]
    reduce_sum x5 -> x0, other arithmetic: 18.2 us -> none  [the longest x3 14.4 us: summed_on_arrival(): return jnp.sum(tiles, axis=0)]
  transfers between devices with their start and end apart: 7 -> 3, of which waited for: 7 -> 1; matrix products, arithmetic and copies ran while one was open for 1% -> 25% of each run, Pallas kernels for 0% -> 60%
where the time goes in v1:
time: 258 us
  Pallas kernels  154 us (60%)
  matrix products  50.3 us (19%)
  other arithmetic  21.7 us (8%)
  local copies, waits for them, and re-layouts  21.2 us (8%)
  waiting for transfers between devices  5.4 us (2%)
  starting transfers between devices  3.92 us (2%)
    pallas_call x1, Pallas kernels, gather_panels(): pl.pallas_call(gather_kernel, out_shape=[jax.ShapeDtypeStruct((3, PANEL,...  102 us
    pallas_call x1, Pallas kernels, inverse_cholesky(): pl.pallas_call(factor_kernel, out_shape=jax.ShapeDtypeStruct((size, size)...  52.4 us
    dot_general x7, matrix products, product(): lax.dot_general(a, b, (((1,), (1,)), ((), ())), precision=precision, pref...  50.3 us
    unnamed x10, local copies, waits for them, and re-layouts  11.2 us
    add x1, other arithmetic, per_device(): here = kept + raw  6.07 us
    ppermute x1, waiting for transfers between devices, per_device(): got = lax.ppermute(sent, 'depth', swap)  5.4 us
    select_n x1, local copies, waits for them, and re-layouts, per_device(): jnp.where(d == 0, jnp.stack([own, peer]), jnp.stack([peer, own]))  5.39 us
  transfers between devices with their start and end apart: 3, of which 1 were waited for; matrix products, arithmetic and copies ran while one was open for 25% of the time, Pallas kernels for 60%

profile of v1, /device:TPU:1, one launch (start us, length us, event | category | flops | bytes accessed | tf_op | source)
XLA Modules:
  0.0 257.6 jit_solution(12276175699024512650)
XLA Ops:
  0.6 4.6 %dynamic-slice_bitcast_fusion = f32[512,2048]{1,0:T(8,128)} fusion(f32[1,1024,4096]{2,1,0:T(8,128)} %param.1, s32[]{:T(128)S(6)} %select_n.105, s32[]{:T(128)S(6)} %select_n.106), kind=kLoop, calls=%fused_computation.11 | loop fusion | bytes 8388616 | tf_op jit(solution)/shard_map/dynamic_slice | solution.py:391
  5.3 1.4 collective-permute-start.1
  6.7 5.8 %copy-done = f32[1,1024,4096]{2,1,0:T(8,128)S(1)} copy-done((f32[1,1024,4096]{2,1,0:T(8,128)S(1)}, f32[1,1024,4096]{2,1,0:T(8,128)}, u32[]{:S(2)}) %copy-start) | copy-done | bytes 16777240
  12.4 101.9 %gather.1 = (f32[3,512,512]{2,1,0:T(8,128)S(1)}, f32[4,4,128,1024]{3,2,1,0:T(8,128)S(1)}, f32[2,512,512]{2,1,0:T(8,128)S(1)}) custom-call(f32[1024,4096]{1,0:T(8,128)S(1)} %bitcast.24), custom_call_target="tpu_custom_call" | custom-call | tf_op jit(solution)/shard_map/gather/pallas_call | solution.py:326
  114.4 3.4 %copy-done.3 = f32[4,4,128,1024]{3,2,1,0:T(8,128)} copy-done((f32[4,4,128,1024]{3,2,1,0:T(8,128)}, f32[4,4,128,1024]{3,2,1,0:T(8,128)S(1)}, u32[]{:S(2)}) %copy-start.3) | copy-done | bytes 8388632
  117.8 52.4 %factor.1 = f32[1024,1024]{1,0:T(8,128)S(1)} custom-call(f32[3,512,512]{2,1,0:T(8,128)S(1)} %get-tuple-element.6.d_ref), custom_call_target="tpu_custom_call" | custom-call | tf_op jit(solution)/shard_map/factor/pallas_call | solution.py:94
  170.2 2.0 copy-done.1
  172.2 3.1 %fusion.27 = f32[512,512]{0,1:T(8,128)S(1)} fusion(f32[1024,1024]{1,0:T(8,128)} %copy-done.1, f32[2,512,512]{2,1,0:T(8,128)S(1)} %get-tuple-element.5), kind=kOutput, calls=%fused_computation.35 | convolution fusion | flops 1610612736 | bytes 3145728 | tf_op jit(solution)/shard_map/dot_general | solution.py:351
  175.3 3.1 %fusion.23 = f32[512,512]{0,1:T(8,128)S(1)} fusion(f32[512,512]{0,1:T(8,128)S(1)} %fusion.27, f32[2,512,512]{2,1,0:T(8,128)S(1)} %get-tuple-element.5, f32[1024,1024]{1,0:T(8,128)} %copy-done.1, pred[]{:T(512)S(6)} %ge.3), kind=kOutput, calls=%fused_computation.29 | convolution fusion | flops 1611137024 | bytes 4194305 | tf_op jit(solution)/shard_map/dot_general | solution.py:351
  178.4 3.1 %fusion.29 = f32[512,512]{0,1:T(8,128)S(1)} fusion(f32[1024,1024]{1,0:T(8,128)} %copy-done.1, f32[2,512,512]{2,1,0:T(8,128)S(1)} %get-tuple-element.5), kind=kOutput, calls=%fused_computation.37 | convolution fusion | flops 1610612736 | bytes 3145728 | tf_op jit(solution)/shard_map/dot_general | solution.py:351
  181.5 1.9 fusion.51
  183.4 2.5 collective-permute-start
  185.9 5.9 %fusion.4 = f32[2048,512]{1,0:T(8,128)S(1)} fusion(f32[2048,1024]{1,0:T(8,128)} %bitcast.25, f32[1024,1024]{1,0:T(8,128)} %copy-done.1), kind=kOutput, calls=%fused_computation.7 | convolution fusion | flops 3221225472 | bytes 9437184 | tf_op jit(solution)/shard_map/dot_general | solution.py:351
  191.8 7.3 %fusion.13 = f32[2048,512]{1,0:T(8,128)} fusion(f32[2048,1024]{1,0:T(8,128)} %bitcast.26, f32[1024,1024]{1,0:T(8,128)S(1)} %copy-done.2), kind=kOutput, calls=%fused_computation.20 | convolution fusion | flops 3221225472 | bytes 9437184 | tf_op jit(solution)/shard_map/dot_general | solution.py:351
  199.1 7.4 %fusion.17 = f32[2048,512]{1,0:T(8,128)} fusion(f32[2048,512]{1,0:T(8,128)S(1)} %fusion.4, f32[2048,1024]{1,0:T(8,128)} %bitcast.27, f32[1024,1024]{1,0:T(8,128)S(1)} %copy-done.2), kind=kOutput, calls=%fused_computation.22 | convolution fusion | flops 3222274048 | bytes 13631488 | tf_op jit(solution)/shard_map/dot_general | solution.py:351
  206.5 5.0 %maximum_select_fusion.3 = f32[2,512,1024]{1,2,0:T(8,128)} fusion(f32[1,512,1024]{1,2,0:T(8,128)} %bitcast.4, f32[1,512,1024]{1,2,0:T(8,128)S(1)} %get-tuple-element.12, pred[]{:T(512)S(6)} %eq.2), kind=kLoop, calls=%fused_computation.9 | loop fusion | flops 3145728 | bytes 8388609 | tf_op jit(solution)/shard_map/jit(_where)/select_n | solution.py:375
  211.5 5.4 %copy.3 = f32[2,512,1024]{2,1,0:T(8,128)} copy(f32[2,512,1024]{1,2,0:T(8,128)} %maximum_select_fusion.3) | data formatting | bytes 8388608 | tf_op jit(solution)/shard_map/jit(_where)/select_n | solution.py:375
  216.9 20.4 %bitcast_subtract_fusion = f32[1024,2048]{1,0:T(8,128)} fusion(f32[1,1024,4096]{2,1,0:T(8,128)} %param.1, s32[]{:T(128)S(6)} %select_n.99, f32[2048,512]{1,0:T(8,128)} %fusion.17, f32[2048,512]{1,0:T(8,128)} %fusion.13, s32[1024]{0:T(1024)S(1)} %get-tuple-element.14, s32[2048]{0:T(1024)S(1)} %fusion.42, f32[1024,1024]{1,0:T(8,128)} %bitcast.28, ...), kind=kOutput, calls=%fused_computation.5 | convolution fusion | flops 12895387648 | bytes 29380612 | tf_op jit(solution)/shard_map/dot_general | solution.py:351
  237.3 6.1 %dynamic-slice_add_fusion = (f32[512,2048]{1,0:T(8,128)S(1)}, f32[512,2048]{1,0:T(8,128)S(1)}) fusion(f32[512,2048]{1,0:T(8,128)} %collective-permute-done.1, f32[1024,2048]{1,0:T(8,128)} %bitcast_subtract_fusion, s32[]{:T(128)S(6)} %select_n.104, s32[]{:T(128)S(6)} %select_n.105), kind=kLoop, calls=%fused_computation.12 | loop fusion | flops 1048576 | bytes 20971528 | tf_op jit(solution)/shard_map/add | solution.py:398
  243.5 0.3 fusion.25
  243.7 1.5 pad_maximum_fusion.1
  245.2 5.4 %collective-permute-done.2 = f32[512,2048]{1,0:T(8,128)S(1)} collective-permute-done((f32[512,2048]{1,0:T(8,128)S(1)}, f32[512,2048]{1,0:T(8,128)S(1)}, u32[]{:S(2)}, u32[]{:S(2)}) %collective-permute-start.2) | collective-permute-done | bytes 4194336 | tf_op jit(solution)/shard_map/ppermute | solution.py:397
  250.6 2.9 %bitcast_add_fusion = f32[512,2048]{1,0:T(8,128)S(1)} fusion(f32[512,2048]{1,0:T(8,128)S(1)} %collective-permute-done.2, f32[1,1024,4096]{2,1,0:T(8,128)} %param.1, s32[]{:T(128)S(6)} %select_n.104, s32[]{:T(128)S(6)} %select_n.106), kind=kLoop, calls=%fused_computation.10 | loop fusion | flops 1048576 | bytes 12582920 | tf_op jit(solution)/shard_map/add | solution.py:399
  253.5 4.1 %maximum_select_fusion.2 = f32[512,4096]{1,0:T(8,128)} fusion(f32[512,2048]{1,0:T(8,128)S(1)} %bitcast_add_fusion, f32[512,2048]{1,0:T(8,128)S(1)} %get-tuple-element.8, pred[]{:T(512)S(6)} %eq.2), kind=kLoop, calls=%fused_computation.4 | loop fusion | flops 6291456 | bytes 16777216 | tf_op jit(solution)/shard_map/jit(_where)/select_n | solution.py:400
  (12 shorter events, 0.1 us)
Async XLA Ops:
  5.3 232.0 %collective-permute-start.1 = (f32[512,2048]{1,0:T(8,128)}, f32[512,2048]{1,0:T(8,128)}, u32[]{:S(2)}, u32[]{:S(2)}) collective-permute-start(f32[512,2048]{1,0:T(8,128)} %dynamic-slice_bitcast_fusion), channel_id=1, source_target_pairs={{0,1},{1,0},{2,3},{3,2},{4,5},{5,4},{6,7},{7,6},{8,9},{9,8},{10,11... | collective-permute-start | bytes 12582920 | tf_op jit(solution)/shard_map/ppermute | solution.py:393
  6.7 5.8 %copy-start = (f32[1,1024,4096]{2,1,0:T(8,128)S(1)}, f32[1,1024,4096]{2,1,0:T(8,128)}, u32[]{:S(2)}) copy-start(f32[1,1024,4096]{2,1,0:T(8,128)} %param.1) | copy-start | bytes 50331652
  114.4 3.4 %copy-start.3 = (f32[4,4,128,1024]{3,2,1,0:T(8,128)}, f32[4,4,128,1024]{3,2,1,0:T(8,128)S(1)}, u32[]{:S(2)}) copy-start(f32[4,4,128,1024]{3,2,1,0:T(8,128)S(1)} %get-tuple-element.7) | copy-start | bytes 25165828
  170.2 2.0 copy-start.1
  183.4 23.1 %collective-permute-start = (f32[512,1024]{0,1:T(8,128)}, f32[512,1024]{0,1:T(8,128)}, u32[]{:S(2)}, u32[]{:S(2)}) collective-permute-start(f32[512,1024]{0,1:T(8,128)} %get-tuple-element.13), channel_id=1, source_target_pairs={{0,1},{1,0},{2,3},{3,2},{4,5},{5,4},{6,7},{7,6},{8,9},{9,8},{10,11... | collective-permute-start | bytes 6291464 | tf_op jit(solution)/shard_map/ppermute | solution.py:374
  185.8 6.0 %copy-start.2 = (f32[1024,1024]{1,0:T(8,128)S(1)}, f32[1024,1024]{1,0:T(8,128)}, u32[]{:S(2)}) copy-start(f32[1024,1024]{1,0:T(8,128)} %copy-done.1) | copy-start | bytes 12582916
  237.3 6.2 %copy-start.4 = (f32[2,512,1024]{2,1,0:T(8,128)S(1)}, f32[2,512,1024]{2,1,0:T(8,128)}, u32[]{:S(2)}) copy-start(f32[2,512,1024]{2,1,0:T(8,128)} %copy.3) | copy-start | bytes 12582916
  243.4 7.2 %collective-permute-start.2 = (f32[512,2048]{1,0:T(8,128)S(1)}, f32[512,2048]{1,0:T(8,128)S(1)}, u32[]{:S(2)}, u32[]{:S(2)}) collective-permute-start(f32[512,2048]{1,0:T(8,128)S(1)} %get-tuple-element.9), channel_id=1, source_target_pairs={{0,1},{1,0},{2,3},{3,2},{4,5},{5,4},{6,7},{7,6},{8,9},{9,8},{10,11... | collective-permute-start | bytes 12582920 | tf_op jit(solution)/shard_map/ppermute | solution.py:397

commit v2 on v1

--- a/solution.py
+++ b/solution.py
@@ -10,6 +10,7 @@
 HI = lax.Precision.HIGHEST
 MESH = pl.DeviceIdType.MESH
 F32 = jnp.float32
+BF16 = jnp.bfloat16
 
 
 def inverse_factor(x):
@@ -50,11 +51,12 @@
     return jnp.concatenate(out, axis=0)
 
 
-def factor_steps(v_ref, urow):
+def factor_steps(v_ref, urow, between):
     size = v_ref.shape[0]
     blocks = size // BLOCK
 
     def step(j, carry):
+        between(j)
         off = pl.multiple_of(j * BLOCK, BLOCK)
         here = pl.ds(off, BLOCK)
         w = inverse_factor(v_ref[here, here])
@@ -81,34 +83,31 @@
     lax.fori_loop(0, blocks, step, 0)
 
 
-def factor_kernel(d_ref, v_ref, urow):
-    v_ref[:PANEL, :PANEL] = d_ref[0]
-    v_ref[:PANEL, PANEL:] = d_ref[1]
-    v_ref[PANEL:, :PANEL] = jnp.zeros((PANEL, PANEL), F32)
-    v_ref[PANEL:, PANEL:] = d_ref[2]
-    factor_steps(v_ref, urow)
-
-
-def inverse_cholesky(d):
-    size = 2 * PANEL
-    return pl.pallas_call(
-        factor_kernel,
-        out_shape=jax.ShapeDtypeStruct((size, size), F32),
-        in_specs=[pl.BlockSpec(memory_space=pltpu.VMEM)],
-        out_specs=pl.BlockSpec(memory_space=pltpu.VMEM),
-        scratch_shapes=[pltpu.VMEM((BLOCK, size), F32)],
-        compiler_params=pltpu.CompilerParams(vmem_limit_bytes=32 * 2**20),
-        name="factor",
-    )(d)
+def product(a, b, precision):
+    return lax.dot_general(a, b, (((1,), (1,)), ((), ())), precision=precision, preferred_element_type=F32)
+
+
+def split(a):
+    high = a.astype(BF16)
+    return high, (a - high.astype(F32)).astype(BF16)
+
+
+def three(ah, al, bh, bl):
+    low = product(ah, bl, None) + product(al, bh, None)
+    return product(ah, bh, None) + low
 
 
 ORDERS = ((2, 1, 0), (0, 2, 1), (1, 0, 2))
+LEADS = ((0, 0), (0, PANEL), (PANEL, PANEL))
 SOURCES = ((0, 0, 0), (0, 0, 1), (1, 0, 1))
 
 
-def gather_kernel(layer, d_out, g_out, o_out, theirs, q, sem):
+def panels_kernel(
+    layer, rows_out, high_out, low_out, raw_out, got_out,
+    v, urow, g_out, o_out, theirs, q, sent, vh, vl, peer_h, peer_l, sem,
+):
     (swap_s, swap_r, half_s, dsc_s, dsc_r, dph_s, dph_r, dsw_s, dsw_r,
-     sc_s, sc_r, own_s, own_r, ag_s, ag_r) = sem
+     sc_s, sc_r, own_s, own_r, ag_s, ag_r, raw_s, raw_r, got_s, got_r, row_s, row_r, near_s) = sem
     r = lax.axis_index("row")
     z = lax.axis_index("col")
     d = lax.axis_index("depth")
@@ -140,6 +139,15 @@
     swap.wait()
     q[...] = q[...] + theirs[...]
 
+    width = 4 * PANEL
+    near = pl.ds(pl.multiple_of(d * width, width), width)
+    far = pl.ds(pl.multiple_of((1 - d) * width, width), width)
+    v[PANEL:, :PANEL] = jnp.zeros((PANEL, PANEL), F32)
+
+    def lead(b, rows, columns):
+        down, right = LEADS[b]
+        return v.at[pl.ds(rows[0] + down, rows[1]), pl.ds(pl.multiple_of(columns + right, PANEL // 2), PANEL // 2)]
+
     half = PANEL // 2
     for b in range(3):
         sx, sy, sz = SOURCES[b]
@@ -154,17 +162,19 @@
                 c[a1] = lax.rem(piece, 4)
                 c[a2] = lax.rem(lax.div(piece, 4), 4)
                 c[a3] = lax.div(piece, 16)
-                rows = pl.ds(pl.multiple_of(piece * 8, 8), 8)
+                first = pl.multiple_of(piece * 8, 8)
+                rows = pl.ds(first, 8)
                 part = pl.ds(pl.multiple_of(depth * half, half), half)
+                target = lead(b, (first, 8), depth * half)
                 own = (c[0] == sx) & (c[1] == sy) & (c[2] == sz) & (depth == 0)
 
                 @pl.when(jnp.logical_not(own))
                 def _():
-                    remote(q.at[rows, part], d_out.at[b, rows, part], dsc_s.at[b], dsc_r.at[b], device(c, depth)).start()
+                    remote(q.at[rows, part], target, dsc_s.at[b], dsc_r.at[b], device(c, depth)).start()
 
                 @pl.when(own)
                 def _():
-                    pltpu.make_async_copy(q.at[rows, part], d_out.at[b, rows, part], dsc_r.at[b]).start()
+                    pltpu.make_async_copy(q.at[rows, part], target, dsc_r.at[b]).start()
 
                 return carry
 
@@ -200,7 +210,7 @@
 
     def phase_copy(b, phase, by):
         start, rows = region(b, phase)
-        ref = d_out.at[b, pl.ds(pl.multiple_of(start, rows), rows), part]
+        ref = lead(b, (pl.multiple_of(start, rows), rows), d * half)
         return remote(
             ref, ref, dph_s.at[b, phase, by - 1], dph_r.at[b, phase, by - 1], device(moved(ORDERS[b][phase], by), d)
         )
@@ -209,7 +219,7 @@
         return pltpu.make_async_copy(ref, ref, s)
 
     for b in range(3):
-        sized(d_out.at[b, pl.ds(0, 8), pl.ds(0, half)], dsc_r.at[b]).wait()
+        sized(urow.at[pl.ds(0, 8), pl.ds(0, half)], dsc_r.at[b]).wait()
         for by in (1, 2, 3):
             phase_copy(b, 0, by).start()
     for phase in (1, 2):
@@ -222,7 +232,7 @@
         for by in (1, 2, 3):
             phase_copy(b, 2, by).wait_recv()
 
-        ref = d_out.at[b, :, part]
+        ref = lead(b, (0, PANEL), d * half)
         remote(ref, ref, dsw_s.at[b], dsw_r.at[b], device(here, 1 - d)).start()
 
     def own_copy(p, to, slot):
@@ -238,7 +248,7 @@
             own_copy(p, 3 - p, 1).start()
 
     for b in range(3):
-        ref = d_out.at[b, :, part]
+        ref = lead(b, (0, PANEL), d * half)
         remote(ref, ref, dsw_s.at[b], dsw_r.at[b], device(here, 1 - d)).wait()
         for phase in range(3):
             for by in (1, 2, 3):
@@ -272,32 +282,100 @@
         sized(g_out.at[0, 0, :, pl.ds(0, PANEL)], sc_r.at[h]).wait()
         for way in range(2):
             ag_copy(h, 0, 0, way).start()
-    for phase in range(2):
+    remote(layer.at[other, far], raw_out, raw_s, raw_r, device(here, 1 - d)).start()
+    pltpu.make_async_copy(layer.at[other, near], sent, near_s).start()
+
+    def received(phase, stage):
         for h in range(2):
             for way in range(2):
-                ag_copy(h, phase, 0, way).wait_recv()
-            for way in range(2):
-                ag_copy(h, phase, 1, way).start()
+                ag_copy(h, phase, stage, way).wait_recv()
+
+    def started(phase, stage):
         for h in range(2):
             for way in range(2):
-                ag_copy(h, phase, 1, way).wait_recv()
-            if phase == 0:
-                for way in range(2):
-                    ag_copy(h, 1, 0, way).start()
-        if phase == 0:
-            for p in range(2):
-
-                @pl.when(z == 3 - p)
-                def _():
-                    sized(o_out.at[p], own_r.at[p]).wait()
-                    ref = o_out.at[p]
-                    remote(ref, ref, own_s.at[0], own_r.at[p], device((x, y, 2 + p), d)).start()
+                ag_copy(h, phase, stage, way).start()
+
+    def between(j):
+        @pl.when(j == 1)
+        def _():
+            received(0, 0)
+            started(0, 1)
+
+        @pl.when(j == 2)
+        def _():
+            received(0, 1)
+            started(1, 0)
+
+        for p in range(2):
+
+            @pl.when((j == 4) & (z == 3 - p))
+            def _():
+                sized(o_out.at[p], own_r.at[p]).wait()
+                ref = o_out.at[p]
+                remote(ref, ref, own_s.at[0], own_r.at[p], device((x, y, 2 + p), d)).start()
+
+        @pl.when(j == 6)
+        def _():
+            received(1, 0)
+            started(1, 1)
+
+    factor_steps(v, urow, between)
+    vh[...] = v[...].astype(BF16)
+    vl[...] = (v[...] - vh[...].astype(F32)).astype(BF16)
 
     for p in range(2):
 
         @pl.when(z != 3 - p)
         def _():
             sized(o_out.at[p], own_r.at[p]).wait()
+
+    c0 = product(o_out[0], v[:PANEL, :PANEL], HI)
+    c1 = product(o_out[0], v[PANEL:, :PANEL], HI) + product(o_out[1], v[PANEL:, PANEL:], HI)
+    rows_out[mine, :PANEL] = c0
+    rows_out[mine, PANEL:] = jnp.where(r + 16 * d >= 1, c1, 0.0)
+    rows = remote(rows_out.at[mine, :], rows_out.at[mine, :], row_s, row_r, device(here, 1 - d))
+    rows.start()
+
+    received(1, 1)
+
+    def solve(k, carry):
+        a = g_out[k].reshape(PANEL, 2 * PANEL)
+        ah, al = split(a)
+        here = pl.ds(pl.multiple_of(k * PANEL, PANEL), PANEL)
+        block = (k + 4 * d) * 4 + z
+        for p in range(2):
+            depth = slice(0, (p + 1) * PANEL)
+            out = slice(p * PANEL, (p + 1) * PANEL)
+            c = three(ah[:, depth], al[:, depth], vh[out, depth], vl[out, depth])
+            ch, cl = split(jnp.where(block > p, c, 0.0))
+            high_out[here, out] = ch
+            low_out[here, out] = cl
+        return carry
+
+    lax.fori_loop(0, 4, solve, 0)
+
+    rows.wait()
+    for p in range(2):
+        out = slice(p * PANEL, (p + 1) * PANEL)
+        ch, cl = split(jnp.where(r + 16 * (1 - d) > p, rows_out[other, out], 0.0))
+        peer_h[:, out] = ch
+        peer_l[:, out] = cl
+    pltpu.make_async_copy(layer.at[other, near], sent, near_s).wait()
+
+    def got_copy(k):
+        tile = pl.ds(pl.multiple_of(k * PANEL, PANEL), PANEL)
+        return remote(sent.at[:, tile], got_out.at[:, tile], got_s.at[k], got_r.at[k], device(here, 1 - d))
+
+    def update(k, carry):
+        tile = pl.ds(pl.multiple_of(k * PANEL, PANEL), PANEL)
+        sent[:, tile] -= three(peer_h[...], peer_l[...], high_out[tile, :], low_out[tile, :])
+        got_copy(k).start()
+        return carry
+
+    lax.fori_loop(0, 4, update, 0)
+    for k in range(4):
+        got_copy(k).wait()
+    remote(layer.at[other, far], raw_out, raw_s, raw_r, device(here, 1 - d)).wait()
 
     for h in range(2):
         for phase in range(2):
@@ -321,83 +399,116 @@
             sized(q.at[pl.ds(0, BLOCK), :], sc_s.at[k]).wait()
 
 
-def gather_panels(layer):
+def panels(layer):
     dma = pltpu.SemaphoreType.DMA
+    width = 4 * PANEL
+    size = 2 * PANEL
+    vmem = pl.BlockSpec(memory_space=pltpu.VMEM)
+    hbm = pl.BlockSpec(memory_space=pltpu.HBM)
     return pl.pallas_call(
-        gather_kernel,
+        panels_kernel,
         out_shape=[
-            jax.ShapeDtypeStruct((3, PANEL, PANEL), F32),
-            jax.ShapeDtypeStruct((4, 4, BLOCK, 2 * PANEL), F32),
-            jax.ShapeDtypeStruct((2, PANEL, PANEL), F32),
+            jax.ShapeDtypeStruct((size, size), F32),
+            jax.ShapeDtypeStruct((width, size), BF16),
+            jax.ShapeDtypeStruct((width, size), BF16),
+            jax.ShapeDtypeStruct((PANEL, width), F32),
+            jax.ShapeDtypeStruct((PANEL, width), F32),
         ],
-        in_specs=[pl.BlockSpec(memory_space=pl.ANY)],
-        out_specs=[
-            pl.BlockSpec(memory_space=pltpu.VMEM),
-            pl.BlockSpec(memory_space=pl.ANY),
-            pl.BlockSpec(memory_space=pl.ANY),
-        ],
+        in_specs=[hbm],
+        out_specs=[vmem, vmem, vmem, hbm, hbm],
         scratch_shapes=[
+            pltpu.VMEM((size, size), F32),
+            pltpu.VMEM((BLOCK, size), F32),
+            pltpu.VMEM((4, 4, BLOCK, size), F32),
+            pltpu.VMEM((2, PANEL, PANEL), F32),
             pltpu.VMEM((PANEL, PANEL), F32),
             pltpu.VMEM((PANEL, PANEL), F32),
+            pltpu.VMEM((PANEL, width), F32),
+            pltpu.VMEM((size, size), BF16),
+            pltpu.VMEM((size, size), BF16),
+            pltpu.VMEM((PANEL, size), BF16),
+            pltpu.VMEM((PANEL, size), BF16),
             (dma, dma, dma, dma((3,)), dma((3,)), dma((3, 3, 3)), dma((3, 3, 3)), dma((3,)), dma((3,)),
-             dma((4,)), dma((2,)), dma((2,)), dma((2,)), dma((16,)), dma((16,))),
+             dma((4,)), dma((2,)), dma((2,)), dma((2,)), dma((16,)), dma((16,)),
+             dma, dma, dma((4,)), dma((4,)), dma, dma, dma),
         ],
-        compiler_params=pltpu.CompilerParams(has_side_effects=True, vmem_limit_bytes=24 * 2**20),
-        name="gather",
+        compiler_params=pltpu.CompilerParams(has_side_effects=True, vmem_limit_bytes=60 * 2**20),
+        name="panels",
     )(layer)
 
 
-def product(a, b, precision=lax.Precision.HIGH):
-    return lax.dot_general(a, b, (((1,), (1,)), ((), ())), precision=precision, preferred_element_type=F32)
-
-
-def solved(a0, a1, v, precision):
-    c0 = product(a0, v[:PANEL, :PANEL], precision)
-    c1 = product(a0, v[PANEL:, :PANEL], precision) + product(a1, v[PANEL:, PANEL:], precision)
-    return c0, c1
+def finish_kernel(info, layer, raw, got, rows_own, rows_all, high, low, schur, factor, own_h, own_l):
+    t = pl.program_id(0)
+    d = info[0]
+    r = info[1]
+
+    @pl.when(t == 0)
+    def _():
+        for p in range(2):
+            out = slice(p * PANEL, (p + 1) * PANEL)
+            ch, cl = split(jnp.where(r + 16 * d > p, rows_own[:, out], 0.0))
+            own_h[:, out] = ch
+            own_l[:, out] = cl
+
+    @pl.when(t < 4)
+    def _():
+        schur[...] = layer[...] + raw[...] - three(own_h[...], own_l[...], high[...], low[...])
+
+    @pl.when(t >= 4)
+    def _():
+        schur[...] = layer[...] + got[...]
+
+    half = PANEL // 2
+    for p in range(2):
+        first = rows_all[:, p * PANEL : p * PANEL + half]
+        factor[p] = jnp.where(d == 0, first, rows_all[:, p * PANEL + half : (p + 1) * PANEL])
+
+
+def finish(info, layer, raw, got, rows, high, low):
+    width = 4 * PANEL
+    size = 2 * PANEL
+
+    def place(t, info):
+        d = info[0]
+        return jnp.where(t < 4, 4 * d + t, 4 * (1 - d) + t - 4)
+
+    def tile(index):
+        return pl.BlockSpec((PANEL, PANEL), index)
+
+    return pl.pallas_call(
+        finish_kernel,
+        out_shape=[
+            jax.ShapeDtypeStruct((PANEL, 2 * width), F32),
+            jax.ShapeDtypeStruct((2, size, PANEL // 2), F32),
+        ],
+        grid_spec=pltpu.PrefetchScalarGridSpec(
+            num_scalar_prefetch=1,
+            grid=(8,),
+            in_specs=[
+                tile(lambda t, info: (info[0], place(t, info))),
+                tile(lambda t, info: (0, jnp.minimum(t, 3))),
+                tile(lambda t, info: (0, jnp.maximum(t - 4, 0))),
+                pl.BlockSpec((PANEL, size), lambda t, info: (info[0], 0)),
+                pl.BlockSpec((BLOCK, size), lambda t, info: (t, 0)),
+                pl.BlockSpec((PANEL, size), lambda t, info: (jnp.minimum(t, 3), 0)),
+                pl.BlockSpec((PANEL, size), lambda t, info: (jnp.minimum(t, 3), 0)),
+            ],
+            out_specs=[
+                tile(lambda t, info: (0, place(t, info))),
+                pl.BlockSpec((2, BLOCK, PANEL // 2), lambda t, info: (0, t, 0)),
+            ],
+            scratch_shapes=[pltpu.VMEM((PANEL, size), BF16), pltpu.VMEM((PANEL, size), BF16)],
+        ),
+        compiler_params=pltpu.CompilerParams(vmem_limit_bytes=40 * 2**20),
+        name="finish",
+    )(info, layer, raw, got, rows, rows, high, low)
 
 
 def per_device(layers):
-    r = lax.axis_index("row")
-    z = lax.axis_index("col")
-    d = lax.axis_index("depth")
     layer = layers[0]
-    lead, column_rows, own_rows = gather_panels(layer)
-    v = inverse_cholesky(lead)
-    g = column_rows.reshape(4 * PANEL, 2 * PANEL)
-    swap = [(0, 1), (1, 0)]
-
-    c0, c1 = solved(own_rows[0], own_rows[1], v, HI)
-    block = r + 16 * d
-    c1 = jnp.where(block >= 1, c1, 0.0)
-    own = jnp.concatenate([c0, c1], axis=1)
-    peer = lax.ppermute(own, "depth", swap)
-    both = jnp.where(d == 0, jnp.stack([own, peer]), jnp.stack([peer, own])).reshape(2 * PANEL, 2 * PANEL)
-    half = PANEL // 2
-    factor = jnp.stack(
-        [jnp.where(d == 0, both[:, p * PANEL : p * PANEL + half], both[:, p * PANEL + half : (p + 1) * PANEL]) for p in range(2)]
-    )
-
-    row_block = jnp.arange(2 * PANEL, dtype=jnp.int32) // PANEL * 16 + r
-    panel = jnp.arange(2 * PANEL, dtype=jnp.int32) // PANEL
-    left = jnp.where(row_block[:, None] > panel[None, :], both, 0.0)
-    k0, k1 = solved(g[:, :PANEL], g[:, PANEL:], v, lax.Precision.HIGH)
-    col_block = (jnp.arange(4 * PANEL, dtype=jnp.int32) // PANEL + 4 * d) * 4 + z
-    right = jnp.where(col_block[:, None] > panel[None, :], jnp.concatenate([k0, k1], axis=1), 0.0)
-
-    width = 4 * PANEL
-    near = lax.dynamic_slice_in_dim(layer, d * width, width, 1)
-    rows_peer = (1 - d) * PANEL
-    far_peer = lax.dynamic_slice(layer, (rows_peer, (1 - d) * width), (PANEL, width))
-    far_mine = lax.dynamic_slice(layer, (d * PANEL, (1 - d) * width), (PANEL, width))
-    raw = lax.ppermute(far_peer, "depth", swap)
-    updated = near - product(left, right)
-    sent = lax.dynamic_slice_in_dim(updated, rows_peer, PANEL, 0)
-    kept = lax.dynamic_slice_in_dim(updated, d * PANEL, PANEL, 0)
-    got = lax.ppermute(sent, "depth", swap)
-    here = kept + raw
-    there = far_mine + got
-    schur = jnp.where(d == 0, jnp.concatenate([here, there], axis=1), jnp.concatenate([there, here], axis=1))
+    info = jnp.stack([lax.axis_index("depth"), lax.axis_index("row")]).astype(jnp.int32)
+    rows, high, low, raw, got = panels(layer)
+    schur, factor = finish(info, layer, raw, got, rows, high, low)
     return factor, schur
 
 

time: 258 us -> 165 us (0.64)
  matrix products: 50.3 us -> 0 us
  other arithmetic: 21.7 us -> 0.08 us
  local copies, waits for them, and re-layouts: 21.2 us -> 6.56 us
  waiting for transfers between devices: 5.4 us -> 0 us
  starting transfers between devices: 3.92 us -> 0 us
  Pallas kernels: 154 us -> 157 us
    dot_general x7 -> x0, matrix products: 50.3 us -> none  [product(): lax.dot_general(a, b, (((1,), (1,)), ((), ())), precision=precision, pref...]
    select_n x3 -> x0, other arithmetic: 9.04 us -> none  [the longest x1 4.99 us: per_device(): jnp.where(d == 0, jnp.stack([own, peer]), jnp.stack([peer, own]))]
    add x3 -> x0, other arithmetic: 9.03 us -> none  [the longest x1 6.07 us: per_device(): here = kept + raw]
    ppermute x3 -> x0, waiting for transfers between devices: 5.4 us -> none  [the longest x1 5.4 us: per_device(): got = lax.ppermute(sent, 'depth', swap)]
    select_n x1 -> x0, local copies, waits for them, and re-layouts: 5.39 us -> none  [per_device(): jnp.where(d == 0, jnp.stack([own, peer]), jnp.stack([peer, own]))]
    unnamed x10 -> x6, local copies, waits for them, and re-layouts: 11.2 us -> 6.56 us
    dynamic_slice x1 -> x0, local copies, waits for them, and re-layouts: 4.64 us -> none  [per_device(): lax.dynamic_slice(layer, (rows_peer, (1 - d) * width), (PANEL, width))]
    ppermute x3 -> x0, starting transfers between devices: 3.92 us -> none  [the longest x1 2.45 us: per_device(): peer = lax.ppermute(own, 'depth', swap)]
  transfers between devices with their start and end apart: 3 -> 0, of which waited for: 1 -> 0; matrix products, arithmetic and copies ran while one was open for 25% -> 0% of each run, Pallas kernels for 60% -> 0%
where the time goes in v2:
time: 165 us; the launch traced here: 164 us
  Pallas kernels  157 us (95%)
  local copies, waits for them, and re-layouts  6.56 us (4%)
    pallas_call x1, Pallas kernels, panels(): pl.pallas_call(panels_kernel, out_shape=[jax.ShapeDtypeStruct((size, size...  140 us
    pallas_call x1, Pallas kernels, finish(): pl.pallas_call(finish_kernel, out_shape=[jax.ShapeDtypeStruct((PANEL, 2 *...  16.5 us
    unnamed x6, local copies, waits for them, and re-layouts  6.56 us

profile of v2, /device:TPU:1, one launch (start us, length us, event | category | flops | bytes accessed | tf_op | source)
XLA Modules:
  0.0 164.2 jit_solution(5369643947026005125)
XLA Ops:
  0.6 0.1 pad_add_fusion.info
  0.7 140.4 %panels.1 = (f32[1024,1024]{1,0:T(8,128)}, bf16[2048,1024]{1,0:T(8,128)(2,1)}, bf16[2048,1024]{1,0:T(8,128)(2,1)}, f32[512,2048]{1,0:T(8,128)}, f32[512,2048]{1,0:T(8,128)}) custom-call(f32[1024,4096]{1,0:T(8,128)} %bitcast.3), custom_call_target="tpu_custom_call" | custom-call | tf_op jit(solution)/shard_map/panels/pallas_call | solution.py:408
  141.2 0.0 copy-start
  141.2 2.2 %copy-done = f32[1024,1024]{1,0:T(8,128)S(1)} copy-done((f32[1024,1024]{1,0:T(8,128)S(1)}, f32[1024,1024]{1,0:T(8,128)}, u32[]{:S(2)}) %copy-start) | copy-done | bytes 4194328
  143.3 0.0 copy-start.1
  143.3 2.2 %copy-done.1 = f32[512,2048]{1,0:T(8,128)S(1)} copy-done((f32[512,2048]{1,0:T(8,128)S(1)}, f32[512,2048]{1,0:T(8,128)}, u32[]{:S(2)}) %copy-start.1) | copy-done | bytes 4194328
  145.5 0.0 copy-start.2
  145.5 2.2 %copy-done.2 = f32[512,2048]{1,0:T(8,128)S(1)} copy-done((f32[512,2048]{1,0:T(8,128)S(1)}, f32[512,2048]{1,0:T(8,128)}, u32[]{:S(2)}) %copy-start.2) | copy-done | bytes 4194328
  147.7 16.5 %finish.1 = (f32[512,4096]{1,0:T(8,128)}, f32[2,1024,256]{2,1,0:T(8,128)}) custom-call(s32[2]{0:T(128)S(1)} %pad_add_fusion.info, f32[1024,4096]{1,0:T(8,128)} %bitcast.4, f32[512,2048]{1,0:T(8,128)S(1)} %copy-done.1, f32[512,2048]{1,0:T(8,128)S(1)} %copy-done.2, f32[1024,1024]{1,0:T(8,128)S(1)} %copy-done, f32[1024,1024]{1,0:T(8,128)S(1)} %copy-done, ...), custom_call_target="tpu_custom_call" | custom-call | tf_op jit(solution)/shard_map/finish/pallas_call | solution.py:478
Async XLA Ops:
  141.2 2.2 %copy-start = (f32[1024,1024]{1,0:T(8,128)S(1)}, f32[1024,1024]{1,0:T(8,128)}, u32[]{:S(2)}) copy-start(f32[1024,1024]{1,0:T(8,128)} %get-tuple-element.11.rows_own.rows_all) | copy-start | bytes 12582916
  143.3 2.2 %copy-start.1 = (f32[512,2048]{1,0:T(8,128)S(1)}, f32[512,2048]{1,0:T(8,128)}, u32[]{:S(2)}) copy-start(f32[512,2048]{1,0:T(8,128)} %get-tuple-element.9.raw) | copy-start | bytes 12582916
  145.5 2.2 %copy-start.2 = (f32[512,2048]{1,0:T(8,128)S(1)}, f32[512,2048]{1,0:T(8,128)}, u32[]{:S(2)}) copy-start(f32[512,2048]{1,0:T(8,128)} %get-tuple-element.10.got) | copy-start | bytes 12582916

commit v3 on v2

--- a/solution.py
+++ b/solution.py
@@ -83,8 +83,8 @@
     lax.fori_loop(0, blocks, step, 0)
 
 
-def product(a, b, precision):
-    return lax.dot_general(a, b, (((1,), (1,)), ((), ())), precision=precision, preferred_element_type=F32)
+def product(a, b, precision, contract=1):
+    return lax.dot_general(a, b, (((1,), (contract,)), ((), ())), precision=precision, preferred_element_type=F32)
 
 
 def split(a):
@@ -92,9 +92,9 @@
     return high, (a - high.astype(F32)).astype(BF16)
 
 
-def three(ah, al, bh, bl):
-    low = product(ah, bl, None) + product(al, bh, None)
-    return product(ah, bh, None) + low
+def three(ah, al, bh, bl, contract=1):
+    low = product(ah, bl, None, contract) + product(al, bh, None, contract)
+    return product(ah, bh, None, contract) + low
 
 
 ORDERS = ((2, 1, 0), (0, 2, 1), (1, 0, 2))
@@ -103,11 +103,11 @@
 
 
 def panels_kernel(
-    layer, rows_out, high_out, low_out, raw_out, got_out,
-    v, urow, g_out, o_out, theirs, q, sent, vh, vl, peer_h, peer_l, sem,
+    layer, rows_hbm, high_hbm, low_hbm, raw_out, got_out,
+    rows_out, high_out, low_out, v, urow, g_out, o_out, theirs, q, sent, vh, vl, peer_h, peer_l, sem,
 ):
-    (swap_s, swap_r, half_s, dsc_s, dsc_r, dph_s, dph_r, dsw_s, dsw_r,
-     sc_s, sc_r, own_s, own_r, ag_s, ag_r, raw_s, raw_r, got_s, got_r, row_s, row_r, near_s) = sem
+    (swap_s, swap_r, half_s, first_s, first_r, second_s, second_r, dph_s, dph_r, dsw_s, dsw_r,
+     sc_s, sc_r, own_s, own_r, ag_s, ag_r, raw_s, raw_r, got_s, got_r, row_s, row_r, near_s, put) = sem
     r = lax.axis_index("row")
     z = lax.axis_index("col")
     d = lax.axis_index("depth")
@@ -149,36 +149,96 @@
         return v.at[pl.ds(rows[0] + down, rows[1]), pl.ds(pl.multiple_of(columns + right, PANEL // 2), PANEL // 2)]
 
     half = PANEL // 2
-    for b in range(3):
-        sx, sy, sz = SOURCES[b]
+
+    def at(b, axes):
+        same = here[axes[0]] == SOURCES[b][axes[0]]
+        for axis in axes[1:]:
+            same = same & (here[axis] == SOURCES[b][axis])
+        return same
+
+    def sized(ref, s):
+        return pltpu.make_async_copy(ref, ref, s)
+
+    def piece(b, stage, t=None):
         a1, a2, a3 = ORDERS[b]
-
-        @pl.when((x == sx) & (y == sy) & (z == sz) & (d == 0))
-        def _():
-            def send(i, carry):
-                c = [None] * 3
-                piece = lax.div(i, 2)
-                depth = lax.rem(i, 2)
-                c[a1] = lax.rem(piece, 4)
-                c[a2] = lax.rem(lax.div(piece, 4), 4)
-                c[a3] = lax.div(piece, 16)
-                first = pl.multiple_of(piece * 8, 8)
-                rows = pl.ds(first, 8)
-                part = pl.ds(pl.multiple_of(depth * half, half), half)
-                target = lead(b, (first, 8), depth * half)
-                own = (c[0] == sx) & (c[1] == sy) & (c[2] == sz) & (depth == 0)
-
-                @pl.when(jnp.logical_not(own))
-                def _():
-                    remote(q.at[rows, part], target, dsc_s.at[b], dsc_r.at[b], device(c, depth)).start()
-
-                @pl.when(own)
-                def _():
-                    pltpu.make_async_copy(q.at[rows, part], target, dsc_r.at[b]).start()
-
-                return carry
-
-            lax.fori_loop(0, 128, send, 0)
+        if stage == 0:
+            return lead(b, (pl.multiple_of(here[a3] * 128, 128), 128), d * half)
+        t = here[a2] if t is None else t
+        return lead(b, (pl.multiple_of(here[a3] * 128 + t * 32, 32), 32), d * half)
+
+    def cut(b, t, depth):
+        c = list(here)
+        c[ORDERS[b][2]] = t
+        src = q.at[pl.ds(128 * t, 128), pl.ds(depth * half, half)]
+        down, right = LEADS[b]
+        dst = v.at[pl.ds(down + 128 * t, 128), pl.ds(right + depth * half, half)]
+        if t == SOURCES[b][ORDERS[b][2]] and depth == 0:
+            return pltpu.make_async_copy(src, dst, first_r.at[b])
+        return remote(src, dst, first_s.at[b, t, depth], first_r.at[b], device(c, depth))
+
+    def cuts(b, act):
+        @pl.when(at(b, (0, 1, 2)) & (d == 0))
+        def _():
+            for t in range(4):
+                for depth in range(2):
+                    if act == "start":
+                        cut(b, t, depth).start()
+                    elif not (t == SOURCES[b][ORDERS[b][2]] and depth == 0):
+                        cut(b, t, depth).wait_send()
+
+    def second(b, t):
+        c = list(here)
+        c[ORDERS[b][1]] = t
+        ref = piece(b, 1, t)
+        return remote(ref, ref, second_s.at[b, t], second_r.at[b], device(c, d))
+
+    def along(b, stage, by):
+        axis = ORDERS[b][stage]
+        ref = piece(b, 0 if stage == 2 else 1)
+        return remote(ref, ref, dph_s.at[b, stage, by - 1], dph_r.at[b, stage, by - 1], device(moved(axis, by), d))
+
+    def copied(b):
+        axis = ORDERS[b][0]
+        for by in (1, 2, 3):
+
+            @pl.when(lax.rem(here[axis] - by + 4, 4) == SOURCES[b][axis])
+            def _():
+                along(b, 0, by).wait_recv()
+
+    def wanted(b, act):
+        a1, a2, a3 = ORDERS[b]
+        for by in (1, 2, 3):
+
+            @pl.when(jnp.logical_not(at(b, (a1,)) & (lax.rem(here[a2] + by, 4) == SOURCES[b][a2])))
+            def _():
+                if act == "start":
+                    along(b, 1, by).start()
+                else:
+                    along(b, 1, by).wait_send()
+
+    for b in range(3):
+        cuts(b, "start")
+    for b in range(3):
+        a1, a2, a3 = ORDERS[b]
+
+        @pl.when(at(b, (a1, a2)))
+        def _():
+            sized(piece(b, 0), first_r.at[b]).wait()
+            for t in range(4):
+                if t != SOURCES[b][a2]:
+                    second(b, t).start()
+
+    for b in range(3):
+        a1, a2, a3 = ORDERS[b]
+
+        @pl.when(at(b, (a1,)))
+        def _():
+            @pl.when(jnp.logical_not(at(b, (a2,))))
+            def _():
+                sized(piece(b, 1), second_r.at[b]).wait()
+
+            for by in (1, 2, 3):
+                along(b, 0, by).start()
 
     for p in range(2):
 
@@ -197,41 +257,20 @@
                 def _():
                     pltpu.make_async_copy(q.at[rows, :], target, sc_r.at[p]).start()
 
-    part = pl.ds(pl.multiple_of(d * half, half), half)
-
-    def region(b, phase):
-        a1, a2, a3 = ORDERS[b]
-        c = here
-        if phase == 0:
-            return c[a3] * 128 + c[a2] * 32 + c[a1] * 8, 8
-        if phase == 1:
-            return c[a3] * 128 + c[a2] * 32, 32
-        return c[a3] * 128, 128
-
-    def phase_copy(b, phase, by):
-        start, rows = region(b, phase)
-        ref = lead(b, (pl.multiple_of(start, rows), rows), d * half)
-        return remote(
-            ref, ref, dph_s.at[b, phase, by - 1], dph_r.at[b, phase, by - 1], device(moved(ORDERS[b][phase], by), d)
-        )
-
-    def sized(ref, s):
-        return pltpu.make_async_copy(ref, ref, s)
-
-    for b in range(3):
-        sized(urow.at[pl.ds(0, 8), pl.ds(0, half)], dsc_r.at[b]).wait()
+    for b in range(3):
+        copied(b)
+        wanted(b, "start")
+    for b in range(3):
+        @pl.when(jnp.logical_not(at(b, ORDERS[b][:2])))
+        def _():
+            for by in (1, 2, 3):
+                along(b, 1, by).wait_recv()
+
         for by in (1, 2, 3):
-            phase_copy(b, 0, by).start()
-    for phase in (1, 2):
-        for b in range(3):
-            for by in (1, 2, 3):
-                phase_copy(b, phase - 1, by).wait_recv()
-            for by in (1, 2, 3):
-                phase_copy(b, phase, by).start()
+            along(b, 2, by).start()
     for b in range(3):
         for by in (1, 2, 3):
-            phase_copy(b, 2, by).wait_recv()
-
+            along(b, 2, by).wait_recv()
         ref = lead(b, (0, PANEL), d * half)
         remote(ref, ref, dsw_s.at[b], dsw_r.at[b], device(here, 1 - d)).start()
 
@@ -250,14 +289,22 @@
     for b in range(3):
         ref = lead(b, (0, PANEL), d * half)
         remote(ref, ref, dsw_s.at[b], dsw_r.at[b], device(here, 1 - d)).wait()
-        for phase in range(3):
+        a1, a2, a3 = ORDERS[b]
+        wanted(b, "wait")
+        for by in (1, 2, 3):
+            along(b, 2, by).wait_send()
+        cuts(b, "wait")
+
+        @pl.when(at(b, (a1, a2)))
+        def _():
+            for t in range(4):
+                if t != SOURCES[b][a2]:
+                    second(b, t).wait_send()
+
+        @pl.when(at(b, (a1,)))
+        def _():
             for by in (1, 2, 3):
-                phase_copy(b, phase, by).wait_send()
-        sx, sy, sz = SOURCES[b]
-
-        @pl.when((x == sx) & (y == sy) & (z == sz) & (d == 0))
-        def _():
-            sized(layer.at[pl.ds(0, 127 * 8), pl.ds(0, half)], dsc_s.at[b]).wait()
+                along(b, 0, by).wait_send()
 
     def ag_ref(h, phase, c, piece):
         cx, cy = c
@@ -320,8 +367,11 @@
             started(1, 1)
 
     factor_steps(v, urow, between)
-    vh[...] = v[...].astype(BF16)
-    vl[...] = (v[...] - vh[...].astype(F32)).astype(BF16)
+    for k in range(4):
+        part = slice(k * 256, (k + 1) * 256)
+        th, tl = split(v[part, :].T)
+        vh[:, part] = th
+        vl[:, part] = tl
 
     for p in range(2):
 
@@ -329,9 +379,8 @@
         def _():
             sized(o_out.at[p], own_r.at[p]).wait()
 
-    c0 = product(o_out[0], v[:PANEL, :PANEL], HI)
+    rows_out[mine, :PANEL] = product(o_out[0], v[:PANEL, :PANEL], HI)
     c1 = product(o_out[0], v[PANEL:, :PANEL], HI) + product(o_out[1], v[PANEL:, PANEL:], HI)
-    rows_out[mine, :PANEL] = c0
     rows_out[mine, PANEL:] = jnp.where(r + 16 * d >= 1, c1, 0.0)
     rows = remote(rows_out.at[mine, :], rows_out.at[mine, :], row_s, row_r, device(here, 1 - d))
     rows.start()
@@ -346,15 +395,27 @@
         for p in range(2):
             depth = slice(0, (p + 1) * PANEL)
             out = slice(p * PANEL, (p + 1) * PANEL)
-            c = three(ah[:, depth], al[:, depth], vh[out, depth], vl[out, depth])
+            c = three(ah[:, depth], al[:, depth], vh[depth, out], vl[depth, out], 0)
             ch, cl = split(jnp.where(block > p, c, 0.0))
             high_out[here, out] = ch
             low_out[here, out] = cl
         return carry
 
+    def put_copies(k):
+        here = pl.ds(pl.multiple_of(k * PANEL, PANEL), PANEL)
+        return (
+            pltpu.make_async_copy(high_out.at[here, :], high_hbm.at[here, :], put.at[k]),
+            pltpu.make_async_copy(low_out.at[here, :], low_hbm.at[here, :], put.at[4 + k]),
+        )
+
     lax.fori_loop(0, 4, solve, 0)
 
     rows.wait()
+    put_rows = pltpu.make_async_copy(rows_out, rows_hbm, put.at[8])
+    put_rows.start()
+    for k in range(4):
+        for copy in put_copies(k):
+            copy.start()
     for p in range(2):
         out = slice(p * PANEL, (p + 1) * PANEL)
         ch, cl = split(jnp.where(r + 16 * (1 - d) > p, rows_out[other, out], 0.0))
@@ -375,6 +436,9 @@
     lax.fori_loop(0, 4, update, 0)
     for k in range(4):
         got_copy(k).wait()
+        for copy in put_copies(k):
+            copy.wait()
+    put_rows.wait()
     remote(layer.at[other, far], raw_out, raw_s, raw_r, device(here, 1 - d)).wait()
 
     for h in range(2):
@@ -403,7 +467,6 @@
     dma = pltpu.SemaphoreType.DMA
     width = 4 * PANEL
     size = 2 * PANEL
-    vmem = pl.BlockSpec(memory_space=pltpu.VMEM)
     hbm = pl.BlockSpec(memory_space=pltpu.HBM)
     return pl.pallas_call(
         panels_kernel,
@@ -415,8 +478,11 @@
             jax.ShapeDtypeStruct((PANEL, width), F32),
         ],
         in_specs=[hbm],
-        out_specs=[vmem, vmem, vmem, hbm, hbm],
+        out_specs=[hbm] * 5,
         scratch_shapes=[
+            pltpu.VMEM((size, size), F32),
+            pltpu.VMEM((width, size), BF16),
+            pltpu.VMEM((width, size), BF16),
             pltpu.VMEM((size, size), F32),
             pltpu.VMEM((BLOCK, size), F32),
             pltpu.VMEM((4, 4, BLOCK, size), F32),
@@ -428,16 +494,16 @@
             pltpu.VMEM((size, size), BF16),
             pltpu.VMEM((PANEL, size), BF16),
             pltpu.VMEM((PANEL, size), BF16),
-            (dma, dma, dma, dma((3,)), dma((3,)), dma((3, 3, 3)), dma((3, 3, 3)), dma((3,)), dma((3,)),
+            (dma, dma, dma, dma((3, 4, 2)), dma((3,)), dma((3, 4)), dma((3,)), dma((3, 3, 3)), dma((3, 3, 3)), dma((3,)), dma((3,)),
              dma((4,)), dma((2,)), dma((2,)), dma((2,)), dma((16,)), dma((16,)),
-             dma, dma, dma((4,)), dma((4,)), dma, dma, dma),
+             dma, dma, dma((4,)), dma((4,)), dma, dma, dma, dma((9,))),
         ],
         compiler_params=pltpu.CompilerParams(has_side_effects=True, vmem_limit_bytes=60 * 2**20),
         name="panels",
     )(layer)
 
 
-def finish_kernel(info, layer, raw, got, rows_own, rows_all, high, low, schur, factor, own_h, own_l):
+def finish_kernel(info, layer, raw, got, rows_own, first, second, high, low, schur, factor, own_h, own_l):
     t = pl.program_id(0)
     d = info[0]
     r = info[1]
@@ -458,10 +524,8 @@
     def _():
         schur[...] = layer[...] + got[...]
 
-    half = PANEL // 2
-    for p in range(2):
-        first = rows_all[:, p * PANEL : p * PANEL + half]
-        factor[p] = jnp.where(d == 0, first, rows_all[:, p * PANEL + half : (p + 1) * PANEL])
+    factor[0] = first[...]
+    factor[1] = second[...]
 
 
 def finish(info, layer, raw, got, rows, high, low):
@@ -489,7 +553,8 @@
                 tile(lambda t, info: (0, jnp.minimum(t, 3))),
                 tile(lambda t, info: (0, jnp.maximum(t - 4, 0))),
                 pl.BlockSpec((PANEL, size), lambda t, info: (info[0], 0)),
-                pl.BlockSpec((BLOCK, size), lambda t, info: (t, 0)),
+                pl.BlockSpec((BLOCK, PANEL // 2), lambda t, info: (t, info[0])),
+                pl.BlockSpec((BLOCK, PANEL // 2), lambda t, info: (t, 2 + info[0])),
                 pl.BlockSpec((PANEL, size), lambda t, info: (jnp.minimum(t, 3), 0)),
                 pl.BlockSpec((PANEL, size), lambda t, info: (jnp.minimum(t, 3), 0)),
             ],
@@ -499,9 +564,9 @@
             ],
             scratch_shapes=[pltpu.VMEM((PANEL, size), BF16), pltpu.VMEM((PANEL, size), BF16)],
         ),
-        compiler_params=pltpu.CompilerParams(vmem_limit_bytes=40 * 2**20),
+        compiler_params=pltpu.CompilerParams(vmem_limit_bytes=60 * 2**20),
         name="finish",
-    )(info, layer, raw, got, rows, rows, high, low)
+    )(info, layer, raw, got, rows, rows, rows, high, low)
 
 
 def per_device(layers):

time: 165 us -> 160 us (0.970)
  local copies, waits for them, and re-layouts: 6.56 us -> 0 us
    unnamed x6 -> x0, local copies, waits for them, and re-layouts: 6.56 us -> none
    pallas_call x1, Pallas kernels: 16.5 us -> 20.1 us  [finish(): pl.pallas_call(finish_kernel, out_shape=[jax.ShapeDtypeStruct((PANEL, 2 *...]
    pallas_call x1, Pallas kernels: 140 us -> 138 us  [panels(): pl.pallas_call(panels_kernel, out_shape=[jax.ShapeDtypeStruct((size, size...]
where the time goes in v3:
time: 160 us; the launch traced here: 159 us
  Pallas kernels  158 us (99%)
    pallas_call x1, Pallas kernels, panels(): pl.pallas_call(panels_kernel, out_shape=[jax.ShapeDtypeStruct((size, size...  138 us
    pallas_call x1, Pallas kernels, finish(): pl.pallas_call(finish_kernel, out_shape=[jax.ShapeDtypeStruct((PANEL, 2 *...  20.1 us

profile of v3, /device:TPU:1, one launch (start us, length us, event | category | flops | bytes accessed | tf_op | source)
XLA Modules:
  0.0 159.1 jit_solution(2025224505385407153)
XLA Ops:
  0.6 0.6 pad_add_fusion.info
  1.2 137.8 %panels.1 = (f32[1024,1024]{1,0:T(8,128)}, bf16[2048,1024]{1,0:T(8,128)(2,1)}, bf16[2048,1024]{1,0:T(8,128)(2,1)}, f32[512,2048]{1,0:T(8,128)}, f32[512,2048]{1,0:T(8,128)}) custom-call(f32[1024,4096]{1,0:T(8,128)} %bitcast.3), custom_call_target="tpu_custom_call" | custom-call | tf_op jit(solution)/shard_map/panels/pallas_call | solution.py:471
  139.0 20.1 %finish.1 = (f32[512,4096]{1,0:T(8,128)}, f32[2,1024,256]{2,1,0:T(8,128)}) custom-call(s32[2]{0:T(128)} %pad_add_fusion.info, f32[1024,4096]{1,0:T(8,128)} %bitcast.4, f32[512,2048]{1,0:T(8,128)} %get-tuple-element.9.raw, f32[512,2048]{1,0:T(8,128)} %get-tuple-element.10.got, f32[1024,1024]{1,0:T(8,128)} %get-tuple-element.11.rows_own.first.second, ...), custom_call_target="tpu_custom_call" | custom-call | tf_op jit(solution)/shard_map/finish/pallas_call | solution.py:542
